TPU v7x, 16 devices: a 4x2x1 block of a 4x4x8 slice. The times are simulated.
16 devices in a mesh: dp: 2 (over y, z), cp: 8 (over x, core).
Axes of the slice: x: 4, y: 2, z: 1, core: 2. Of those that a mesh axis runs over, the one named last changes fastest.
The devices are a block of a 4x4x8 slice.
Arguments:
- hidden: bfloat16 [16384, 2560], P(('dp', 'cp')), parts along dimension 0
- w_query: bfloat16 [6, 2560, 8, 256], replicated
- w_key: bfloat16 [6, 2560, 8, 256], replicated
- w_value: bfloat16 [6, 2560, 8, 256], replicated
- w_out: bfloat16 [6, 8, 256, 2560], replicated
Outputs:
- output: bfloat16 [16384, 2560], P(('dp', 'cp')), parts along dimension 0
There are 2 independent parts. A program takes and returns all parts, laid end to end along the dimension named above; an argument that names none is the same for every part.
All inputs are finite; a program needn't handle non-finite values.
Results may differ from a plain program's by a relative error of at most 0.0121398.
Values are sent between devices in bfloat16 or wider.
A program may use at most 768 MiB of HBM per device.

v0:
```python
import jax
import jax.numpy as jnp
from jax import lax
from jax.sharding import PartitionSpec as P

WINDOW = 1024
NORM_EPS = 1e-6
NEG_BIG = -1e30


def rms_norm(hidden):
    hid_f = hidden.astype(jnp.float32)
    return (hid_f * lax.rsqrt(jnp.mean(hid_f * hid_f, axis=-1, keepdims=True) + NORM_EPS)).astype(jnp.bfloat16)


def project(normed, weight):
    d_model, n_heads, head_dim = weight.shape
    flat_out = jnp.dot(normed, weight.reshape(d_model, n_heads * head_dim), preferred_element_type=jnp.float32)
    return flat_out.astype(jnp.bfloat16).reshape(normed.shape[:-1] + (n_heads, head_dim))


def empty_state(q_blk):
    lead_shape = q_blk.shape[:-1]
    return (jnp.full(lead_shape, NEG_BIG, jnp.float32), jnp.zeros(lead_shape, jnp.float32), jnp.zeros(q_blk.shape, jnp.float32))


def block_update(soft_state, q_blk, k_blk, v_blk, allowed):
    run_max, run_sum, acc_out = soft_state
    scores = jnp.einsum("...qhd,...khd->...qhk", q_blk, k_blk, preferred_element_type=jnp.float32) * (q_blk.shape[-1] ** -0.5)
    scores = jnp.where(allowed, scores, NEG_BIG)
    new_max = jnp.maximum(run_max, jnp.max(scores, axis=-1))
    prob_blk = jnp.where(allowed, jnp.exp(scores - new_max[..., None]), 0.0)
    rescale = jnp.exp(run_max - new_max)
    new_sum = run_sum * rescale + jnp.sum(prob_blk, axis=-1)
    new_acc = acc_out * rescale[..., None] + jnp.einsum("...qhk,...khd->...qhd", prob_blk.astype(jnp.bfloat16), v_blk, preferred_element_type=jnp.float32)
    return new_max, new_sum, new_acc


def finish(soft_state):
    run_max, run_sum, acc_out = soft_state
    return (acc_out / run_sum[..., None]).astype(jnp.bfloat16)


def out_update(hidden, attn_out, weight):
    n_heads, head_dim, d_model = weight.shape
    flat_attn = attn_out.reshape(attn_out.shape[:-2] + (n_heads * head_dim,))
    out_proj = jnp.dot(flat_attn, weight.reshape(n_heads * head_dim, d_model), preferred_element_type=jnp.float32)
    return (hidden.astype(jnp.float32) + out_proj).astype(jnp.bfloat16)


def solution(mesh):
    n_cp = mesh.shape["cp"]

    def device_body(hidden, w_query, w_key, w_value, w_out):
        n_tok = hidden.shape[0]
        n_layers = w_query.shape[0]
        n_back = min((WINDOW + n_tok - 2) // n_tok, n_cp - 1)
        my_rank = lax.axis_index("cp")
        offsets = jnp.arange(n_tok)
        q_pos = my_rank * n_tok + offsets
        own_gap = offsets[:, None] - offsets[None, :]
        local_own = ((own_gap >= 0) & (own_gap < WINDOW))[:, None, :]
        causal_own = (own_gap >= 0)[:, None, :]
        next_pairs = [(src_rank, (src_rank + 1) % n_cp) for src_rank in range(n_cp)]
        for layer_idx in range(n_layers):
            normed = rms_norm(hidden)
            q_loc = project(normed, w_query[layer_idx])
            k_loc = project(normed, w_key[layer_idx])
            v_loc = project(normed, w_value[layer_idx])
            soft_state = empty_state(q_loc)
            if layer_idx < n_layers - 1:
                soft_state = block_update(soft_state, q_loc, k_loc, v_loc, local_own)
                for back_idx in range(1, n_back + 1):
                    n_need = min(n_tok, WINDOW - 1 - (back_idx - 1) * n_tok)
                    shift_pairs = [(src_rank, src_rank + back_idx) for src_rank in range(n_cp - back_idx)]
                    k_halo, v_halo = lax.ppermute((k_loc[n_tok - n_need:], v_loc[n_tok - n_need:]), "cp", shift_pairs)
                    k_pos = (my_rank - back_idx) * n_tok + (n_tok - n_need) + jnp.arange(n_need)
                    allowed = ((q_pos[:, None] - k_pos[None, :] < WINDOW) & (k_pos[None, :] >= 0))[:, None, :]
                    soft_state = block_update(soft_state, q_loc, k_halo, v_halo, allowed)
            else:
                soft_state = block_update(soft_state, q_loc, k_loc, v_loc, causal_own)

                def pass_step(step_idx, loop_state):
                    state_in, k_cur, v_cur = loop_state
                    k_cur, v_cur = lax.ppermute((k_cur, v_cur), "cp", next_pairs)
                    k_pos = ((my_rank - step_idx) % n_cp) * n_tok + offsets
                    allowed = (k_pos[None, :] <= q_pos[:, None])[:, None, :]
                    return block_update(state_in, q_loc, k_cur, v_cur, allowed), k_cur, v_cur

                soft_state, k_last, v_last = lax.fori_loop(1, n_cp, pass_step, (soft_state, k_loc, v_loc))
            hidden = out_update(hidden, finish(soft_state), w_out[layer_idx])
        return hidden

    row_spec = P(("dp", "cp"), None)
    return jax.shard_map(device_body, mesh=mesh, in_specs=(row_spec, P(), P(), P(), P()), out_specs=row_spec, check_vma=False)
```

profile of v0, /device:TPU:113, one launch (start us, length us, event | category | flops | bytes accessed | tf_op | source)
XLA Modules:
  0.0 2834.6 jit_solution(16557091555727765953)
XLA Ops:
  3.6 41.0 %fusion.211 = (bf16[1,2560,8,256]{3,2,1,0:T(8,128)(2,1)}, bf16[1,2560,8,256]{3,2,1,0:T(8,128)(2,1)}, bf16[1,2560,8,256]{3,2,1,0:T(8,128)(2,1)}, bf16[1,2560,8,25...) fusion(bf16[6,2560,8,256]{3,2,1,0:T(8,128)(2,1)} %param.9), kind=kLoop, calls=%fused_computation.299 | loop fusion | bytes 125829120 | tf_op jit(solution)/shard_map/slice | solution.py:68
  83.1 41.3 %fusion.209 = (bf16[1,2560,8,256]{3,2,1,0:T(8,128)(2,1)}, bf16[1,2560,8,256]{3,2,1,0:T(8,128)(2,1)}, bf16[1,2560,8,256]{3,2,1,0:T(8,128)(2,1)}, bf16[1,2560,8,25...) fusion(bf16[6,2560,8,256]{3,2,1,0:T(8,128)(2,1)} %param.10), kind=kLoop, calls=%fused_computation.297 | loop fusion | bytes 125829120 | tf_op jit(solution)/shard_map/slice | solution.py:69
  159.7 41.3 %fusion.210 = (bf16[1,2560,8,256]{3,2,1,0:T(8,128)(2,1)}, bf16[1,2560,8,256]{3,2,1,0:T(8,128)(2,1)}, bf16[1,2560,8,256]{3,2,1,0:T(8,128)(2,1)}, bf16[1,2560,8,25...) fusion(bf16[6,2560,8,256]{3,2,1,0:T(8,128)(2,1)} %param.8), kind=kLoop, calls=%fused_computation.298 | loop fusion | bytes 125829120 | tf_op jit(solution)/shard_map/slice | solution.py:67
  446.2 42.0 %fusion.208 = (bf16[1,8,256,2560]{3,2,1,0:T(8,128)(2,1)}, bf16[1,8,256,2560]{3,2,1,0:T(8,128)(2,1)}, bf16[1,8,256,2560]{3,2,1,0:T(8,128)(2,1)}, bf16[1,8,256,256...) fusion(bf16[6,8,256,2560]{3,2,1,0:T(8,128)(2,1)} %param.11), kind=kLoop, calls=%fused_computation.296 | loop fusion | bytes 125829120 | tf_op jit(solution)/shard_map/slice | solution.py:91
  507.3 35.0 %fusion.43 = f32[1024,8]{0,1:T(8,128)S(1)} fusion(f32[8,1023,1024]{2,1,0:T(8,128)} %fusion.133, pred[1024,1023]{0,1:T(8,128)(4,1)S(1)} %fusion.152), kind=kLoop, calls=%fused_computation.73 | loop fusion | flops 25133056 | bytes 34601984 | tf_op jit(solution)/shard_map/reduce_max | solution.py:31
  734.1 58.2 %collective-permute-done.4 = bf16[1023,8,256]{2,1,0:T(8,128)(2,1)} collective-permute-done((bf16[1023,8,256]{2,1,0:T(8,128)(2,1)}, bf16[1023,8,256]{2,1,0:T(8,128)(2,1)}, u32[]{:S(2)}, u32[]{:S(2)}) %collective-permute-start.4) | collective-permute-done | bytes 4190240 | tf_op jit(solution)/shard_map/ppermute | solution.py:76
  811.4 35.2 %fusion.44 = f32[1024,8]{0,1:T(8,128)S(1)} fusion(f32[8,1023,1024]{2,1,0:T(8,128)} %fusion.127, pred[1024,1023]{0,1:T(8,128)(4,1)S(1)} %copy-done.6), kind=kLoop, calls=%fused_computation.74 | loop fusion | flops 25133056 | bytes 34601984 | tf_op jit(solution)/shard_map/reduce_max | solution.py:31
  903.3 30.1 %fusion.104 = bf16[1024,8,256]{0,2,1:T(8,128)(2,1)} fusion(f32[8,256,1024]{2,1,0:T(8,128)} %fusion.66, f32[1024,8]{0,1:T(8,128)S(1)} %get-tuple-element.335, f32[1024,8]{0,1:T(8,128)S(1)} %get-tuple-element.336, f32[1024,8]{0,1:T(8,128)S(1)} %get-tuple-element.388, bf16[1024,8,1023]{0,1,2:T(8,128)(2,1)} %get-tuple-element.374, ...), kind=kOutput, calls=%fused_computation.154 | convolution fusion | flops 4301258752 | bytes 33632256 | tf_op jit(solution)/shard_map/...qhk,...khd->...qhd/dot_general | solution.py:35
  1039.0 58.0 %collective-permute-done.6 = bf16[1023,8,256]{2,1,0:T(8,128)(2,1)} collective-permute-done((bf16[1023,8,256]{2,1,0:T(8,128)(2,1)}, bf16[1023,8,256]{2,1,0:T(8,128)(2,1)}, u32[]{:S(2)}, u32[]{:S(2)}) %collective-permute-start.6) | collective-permute-done | bytes 4190240 | tf_op jit(solution)/shard_map/ppermute | solution.py:76
  1116.1 35.2 %fusion.45 = f32[1024,8]{0,1:T(8,128)S(1)} fusion(f32[8,1023,1024]{2,1,0:T(8,128)} %fusion.121, pred[1024,1023]{0,1:T(8,128)(4,1)S(1)} %copy-done.7), kind=kLoop, calls=%fused_computation.75 | loop fusion | flops 25133056 | bytes 34601984 | tf_op jit(solution)/shard_map/reduce_max | solution.py:31
  1208.0 29.9 %fusion.101 = bf16[1024,8,256]{0,2,1:T(8,128)(2,1)} fusion(f32[8,256,1024]{2,1,0:T(8,128)} %fusion.64, f32[1024,8]{0,1:T(8,128)S(1)} %get-tuple-element.333, f32[1024,8]{0,1:T(8,128)S(1)} %get-tuple-element.334, f32[1024,8]{0,1:T(8,128)S(1)} %get-tuple-element.385, bf16[1024,8,1023]{0,1,2:T(8,128)(2,1)} %get-tuple-element.372, ...), kind=kOutput, calls=%fused_computation.149 | convolution fusion | flops 4301258752 | bytes 33632256 | tf_op jit(solution)/shard_map/...qhk,...khd->...qhd/dot_general | solution.py:35
  1343.6 58.2 %collective-permute-done.8 = bf16[1023,8,256]{2,1,0:T(8,128)(2,1)} collective-permute-done((bf16[1023,8,256]{2,1,0:T(8,128)(2,1)}, bf16[1023,8,256]{2,1,0:T(8,128)(2,1)}, u32[]{:S(2)}, u32[]{:S(2)}) %collective-permute-start.8) | collective-permute-done | bytes 4190240 | tf_op jit(solution)/shard_map/ppermute | solution.py:76
  1420.9 35.5 %fusion.46 = f32[1024,8]{0,1:T(8,128)S(1)} fusion(f32[8,1023,1024]{2,1,0:T(8,128)} %fusion.115, pred[1024,1023]{0,1:T(8,128)(4,1)S(1)} %copy-done.8), kind=kLoop, calls=%fused_computation.76 | loop fusion | flops 25133056 | bytes 34601984 | tf_op jit(solution)/shard_map/reduce_max | solution.py:31
  1648.3 58.3 %collective-permute-done.10 = bf16[1023,8,256]{2,1,0:T(8,128)(2,1)} collective-permute-done((bf16[1023,8,256]{2,1,0:T(8,128)(2,1)}, bf16[1023,8,256]{2,1,0:T(8,128)(2,1)}, u32[]{:S(2)}, u32[]{:S(2)}) %collective-permute-start.10) | collective-permute-done | bytes 4190240 | tf_op jit(solution)/shard_map/ppermute | solution.py:76
  1725.7 35.2 %fusion.47 = f32[1024,8]{0,1:T(8,128)S(1)} fusion(f32[8,1023,1024]{2,1,0:T(8,128)} %fusion.109, pred[1024,1023]{0,1:T(8,128)(4,1)S(1)} %copy-done.9), kind=kLoop, calls=%fused_computation.77 | loop fusion | flops 25133056 | bytes 34601984 | tf_op jit(solution)/shard_map/reduce_max | solution.py:31
  1817.5 30.0 %fusion.95 = bf16[1024,8,256]{0,2,1:T(8,128)(2,1)} fusion(f32[8,256,1024]{2,1,0:T(8,128)} %fusion.60, f32[1024,8]{0,1:T(8,128)S(1)} %get-tuple-element.329, f32[1024,8]{0,1:T(8,128)S(1)} %get-tuple-element.330, f32[1024,8]{0,1:T(8,128)S(1)} %get-tuple-element.379, bf16[1024,8,1023]{0,1,2:T(8,128)(2,1)} %get-tuple-element.368, ...), kind=kOutput, calls=%fused_computation.139 | convolution fusion | flops 4301258752 | bytes 33632256 | tf_op jit(solution)/shard_map/...qhk,...khd->...qhd/dot_general | solution.py:35
  1981.9 822.2 %while.24 = (s32[]{:T(128)}, f32[1024,8]{0,1:T(8,128)S(1)}, f32[1024,8]{0,1:T(8,128)S(1)}, f32[1024,8,256]{2,0,1:T(8,128)}, bf16[1024,8,256]{2,0,1:T(8,128)(2,1)...) while((s32[]{:T(128)}, f32[1024,8]{0,1:T(8,128)S(1)}, ...), condition=%wide.region_31.32_spmd.clone, body=%wide.region_28.31_spmd.clone.sunk | while | flops 8704247808 | bytes 243810752 | solution.py:90
  1985.1 44.7 %collective-permute-done = bf16[1024,8,256]{2,0,1:T(8,128)(2,1)} collective-permute-done((bf16[1024,8,256]{2,0,1:T(8,128)(2,1)}, bf16[1024,8,256]{2,0,1:T(8,128)(2,1)}, u32[]{:S(2)}, u32[]{:S(2)}) %collective-permute-start) | collective-permute-done | bytes 4194336 | tf_op jit(solution)/shard_map/while/body/eval_jaxpr/ppermute | solution.py:85
  2102.5 44.7 %collective-permute-done = bf16[1024,8,256]{2,0,1:T(8,128)(2,1)} collective-permute-done((bf16[1024,8,256]{2,0,1:T(8,128)(2,1)}, bf16[1024,8,256]{2,0,1:T(8,128)(2,1)}, u32[]{:S(2)}, u32[]{:S(2)}) %collective-permute-start) | collective-permute-done | bytes 4194336 | tf_op jit(solution)/shard_map/while/body/eval_jaxpr/ppermute | solution.py:85
  2220.0 44.7 %collective-permute-done = bf16[1024,8,256]{2,0,1:T(8,128)(2,1)} collective-permute-done((bf16[1024,8,256]{2,0,1:T(8,128)(2,1)}, bf16[1024,8,256]{2,0,1:T(8,128)(2,1)}, u32[]{:S(2)}, u32[]{:S(2)}) %collective-permute-start) | collective-permute-done | bytes 4194336 | tf_op jit(solution)/shard_map/while/body/eval_jaxpr/ppermute | solution.py:85
  2337.4 44.7 %collective-permute-done = bf16[1024,8,256]{2,0,1:T(8,128)(2,1)} collective-permute-done((bf16[1024,8,256]{2,0,1:T(8,128)(2,1)}, bf16[1024,8,256]{2,0,1:T(8,128)(2,1)}, u32[]{:S(2)}, u32[]{:S(2)}) %collective-permute-start) | collective-permute-done | bytes 4194336 | tf_op jit(solution)/shard_map/while/body/eval_jaxpr/ppermute | solution.py:85
  2454.9 44.7 %collective-permute-done = bf16[1024,8,256]{2,0,1:T(8,128)(2,1)} collective-permute-done((bf16[1024,8,256]{2,0,1:T(8,128)(2,1)}, bf16[1024,8,256]{2,0,1:T(8,128)(2,1)}, u32[]{:S(2)}, u32[]{:S(2)}) %collective-permute-start) | collective-permute-done | bytes 4194336 | tf_op jit(solution)/shard_map/while/body/eval_jaxpr/ppermute | solution.py:85
  2572.3 44.7 %collective-permute-done = bf16[1024,8,256]{2,0,1:T(8,128)(2,1)} collective-permute-done((bf16[1024,8,256]{2,0,1:T(8,128)(2,1)}, bf16[1024,8,256]{2,0,1:T(8,128)(2,1)}, u32[]{:S(2)}, u32[]{:S(2)}) %collective-permute-start) | collective-permute-done | bytes 4194336 | tf_op jit(solution)/shard_map/while/body/eval_jaxpr/ppermute | solution.py:85
  2689.8 44.7 %collective-permute-done = bf16[1024,8,256]{2,0,1:T(8,128)(2,1)} collective-permute-done((bf16[1024,8,256]{2,0,1:T(8,128)(2,1)}, bf16[1024,8,256]{2,0,1:T(8,128)(2,1)}, u32[]{:S(2)}, u32[]{:S(2)}) %collective-permute-start) | collective-permute-done | bytes 4194336 | tf_op jit(solution)/shard_map/while/body/eval_jaxpr/ppermute | solution.py:85
  (435 shorter events, 1854.9 us)
Async XLA Ops:
  78.5 409.8 %collective-permute-start.2 = (bf16[1023,8,256]{2,1,0:T(8,128)(2,1)}, bf16[1023,8,256]{2,1,0:T(8,128)(2,1)}, u32[]{:S(2)}, u32[]{:S(2)}) collective-permute-start(bf16[1023,8,256]{2,1,0:T(8,128)(2,1)} %slice.186), channel_id=1, source_target_pairs={{0,1},{1,2},{2,3},{3,4},{4,5},{5,6},{6,7},{8,9},{9,10},{10,11},{11... | collective-permute-start | bytes 12570632 | tf_op jit(solution)/shard_map/ppermute | solution.py:76
  157.4 442.0 %collective-permute-start.3 = (bf16[1023,8,256]{2,1,0:T(8,128)(2,1)}, bf16[1023,8,256]{2,1,0:T(8,128)(2,1)}, u32[]{:S(2)}, u32[]{:S(2)}) collective-permute-start(bf16[1023,8,256]{2,1,0:T(8,128)(2,1)} %slice.187), channel_id=1, source_target_pairs={{0,1},{1,2},{2,3},{3,4},{4,5},{5,6},{6,7},{8,9},{9,10},{10,11},{11... | collective-permute-start | bytes 12570632 | tf_op jit(solution)/shard_map/ppermute | solution.py:76
  698.1 205.1 %collective-permute-start.5 = (bf16[1023,8,256]{2,1,0:T(8,128)(2,1)}, bf16[1023,8,256]{2,1,0:T(8,128)(2,1)}, u32[]{:S(2)}, u32[]{:S(2)}) collective-permute-start(bf16[1023,8,256]{2,1,0:T(8,128)(2,1)} %slice.189), channel_id=1, source_target_pairs={{0,1},{1,2},{2,3},{3,4},{4,5},{5,6},{6,7},{8,9},{9,10},{10,11},{11... | collective-permute-start | bytes 12570632 | tf_op jit(solution)/shard_map/ppermute | solution.py:76
  702.1 90.3 %collective-permute-start.4 = (bf16[1023,8,256]{2,1,0:T(8,128)(2,1)}, bf16[1023,8,256]{2,1,0:T(8,128)(2,1)}, u32[]{:S(2)}, u32[]{:S(2)}) collective-permute-start(bf16[1023,8,256]{2,1,0:T(8,128)(2,1)} %slice.188), channel_id=1, source_target_pairs={{0,1},{1,2},{2,3},{3,4},{4,5},{5,6},{6,7},{8,9},{9,10},{10,11},{11... | collective-permute-start | bytes 12570632 | tf_op jit(solution)/shard_map/ppermute | solution.py:76
  1002.0 205.9 %collective-permute-start.7 = (bf16[1023,8,256]{2,1,0:T(8,128)(2,1)}, bf16[1023,8,256]{2,1,0:T(8,128)(2,1)}, u32[]{:S(2)}, u32[]{:S(2)}) collective-permute-start(bf16[1023,8,256]{2,1,0:T(8,128)(2,1)} %slice.191), channel_id=1, source_target_pairs={{0,1},{1,2},{2,3},{3,4},{4,5},{5,6},{6,7},{8,9},{9,10},{10,11},{11... | collective-permute-start | bytes 12570632 | tf_op jit(solution)/shard_map/ppermute | solution.py:76
  1006.7 90.3 %collective-permute-start.6 = (bf16[1023,8,256]{2,1,0:T(8,128)(2,1)}, bf16[1023,8,256]{2,1,0:T(8,128)(2,1)}, u32[]{:S(2)}, u32[]{:S(2)}) collective-permute-start(bf16[1023,8,256]{2,1,0:T(8,128)(2,1)} %slice.190), channel_id=1, source_target_pairs={{0,1},{1,2},{2,3},{3,4},{4,5},{5,6},{6,7},{8,9},{9,10},{10,11},{11... | collective-permute-start | bytes 12570632 | tf_op jit(solution)/shard_map/ppermute | solution.py:76
  1306.8 206.1 %collective-permute-start.9 = (bf16[1023,8,256]{2,1,0:T(8,128)(2,1)}, bf16[1023,8,256]{2,1,0:T(8,128)(2,1)}, u32[]{:S(2)}, u32[]{:S(2)}) collective-permute-start(bf16[1023,8,256]{2,1,0:T(8,128)(2,1)} %slice.193), channel_id=1, source_target_pairs={{0,1},{1,2},{2,3},{3,4},{4,5},{5,6},{6,7},{8,9},{9,10},{10,11},{11... | collective-permute-start | bytes 12570632 | tf_op jit(solution)/shard_map/ppermute | solution.py:76
  1311.5 90.3 %collective-permute-start.8 = (bf16[1023,8,256]{2,1,0:T(8,128)(2,1)}, bf16[1023,8,256]{2,1,0:T(8,128)(2,1)}, u32[]{:S(2)}, u32[]{:S(2)}) collective-permute-start(bf16[1023,8,256]{2,1,0:T(8,128)(2,1)} %slice.192), channel_id=1, source_target_pairs={{0,1},{1,2},{2,3},{3,4},{4,5},{5,6},{6,7},{8,9},{9,10},{10,11},{11... | collective-permute-start | bytes 12570632 | tf_op jit(solution)/shard_map/ppermute | solution.py:76
  1611.6 205.9 %collective-permute-start.11 = (bf16[1023,8,256]{2,1,0:T(8,128)(2,1)}, bf16[1023,8,256]{2,1,0:T(8,128)(2,1)}, u32[]{:S(2)}, u32[]{:S(2)}) collective-permute-start(bf16[1023,8,256]{2,1,0:T(8,128)(2,1)} %slice.195), channel_id=1, source_target_pairs={{0,1},{1,2},{2,3},{3,4},{4,5},{5,6},{6,7},{8,9},{9,10},{10,11},{11... | collective-permute-start | bytes 12570632 | tf_op jit(solution)/shard_map/ppermute | solution.py:76
  1616.3 90.3 %collective-permute-start.10 = (bf16[1023,8,256]{2,1,0:T(8,128)(2,1)}, bf16[1023,8,256]{2,1,0:T(8,128)(2,1)}, u32[]{:S(2)}, u32[]{:S(2)}) collective-permute-start(bf16[1023,8,256]{2,1,0:T(8,128)(2,1)} %slice.194), channel_id=1, source_target_pairs={{0,1},{1,2},{2,3},{3,4},{4,5},{5,6},{6,7},{8,9},{9,10},{10,11},{11... | collective-permute-start | bytes 12570632 | tf_op jit(solution)/shard_map/ppermute | solution.py:76
  1981.9 47.9 %collective-permute-start = (bf16[1024,8,256]{2,0,1:T(8,128)(2,1)}, bf16[1024,8,256]{2,0,1:T(8,128)(2,1)}, u32[]{:S(2)}, u32[]{:S(2)}) collective-permute-start(bf16[1024,8,256]{2,0,1:T(8,128)(2,1)} %get-tuple-element.503), channel_id=1, source_target_pairs={{0,1},{1,2},{2,3},{3,4},{4,5},{5,6},{6,7},{7,0},{8,9},{9,10},{10,1... | collective-permute-start | bytes 12582920 | tf_op jit(solution)/shard_map/while/body/eval_jaxpr/ppermute | solution.py:85
  1984.4 90.4 %collective-permute-start.1 = (bf16[1024,8,256]{2,0,1:T(8,128)(2,1)}, bf16[1024,8,256]{2,0,1:T(8,128)(2,1)}, u32[]{:S(2)}, u32[]{:S(2)}) collective-permute-start(bf16[1024,8,256]{2,0,1:T(8,128)(2,1)} %get-tuple-element.504), channel_id=1, source_target_pairs={{0,1},{1,2},{2,3},{3,4},{4,5},{5,6},{6,7},{7,0},{8,9},{9,10},{10,1... | collective-permute-start | bytes 12582920 | tf_op jit(solution)/shard_map/while/body/eval_jaxpr/ppermute | solution.py:85
  2099.4 47.9 %collective-permute-start = (bf16[1024,8,256]{2,0,1:T(8,128)(2,1)}, bf16[1024,8,256]{2,0,1:T(8,128)(2,1)}, u32[]{:S(2)}, u32[]{:S(2)}) collective-permute-start(bf16[1024,8,256]{2,0,1:T(8,128)(2,1)} %get-tuple-element.503), channel_id=1, source_target_pairs={{0,1},{1,2},{2,3},{3,4},{4,5},{5,6},{6,7},{7,0},{8,9},{9,10},{10,1... | collective-permute-start | bytes 12582920 | tf_op jit(solution)/shard_map/while/body/eval_jaxpr/ppermute | solution.py:85
  2101.9 90.4 %collective-permute-start.1 = (bf16[1024,8,256]{2,0,1:T(8,128)(2,1)}, bf16[1024,8,256]{2,0,1:T(8,128)(2,1)}, u32[]{:S(2)}, u32[]{:S(2)}) collective-permute-start(bf16[1024,8,256]{2,0,1:T(8,128)(2,1)} %get-tuple-element.504), channel_id=1, source_target_pairs={{0,1},{1,2},{2,3},{3,4},{4,5},{5,6},{6,7},{7,0},{8,9},{9,10},{10,1... | collective-permute-start | bytes 12582920 | tf_op jit(solution)/shard_map/while/body/eval_jaxpr/ppermute | solution.py:85
  2216.8 47.9 %collective-permute-start = (bf16[1024,8,256]{2,0,1:T(8,128)(2,1)}, bf16[1024,8,256]{2,0,1:T(8,128)(2,1)}, u32[]{:S(2)}, u32[]{:S(2)}) collective-permute-start(bf16[1024,8,256]{2,0,1:T(8,128)(2,1)} %get-tuple-element.503), channel_id=1, source_target_pairs={{0,1},{1,2},{2,3},{3,4},{4,5},{5,6},{6,7},{7,0},{8,9},{9,10},{10,1... | collective-permute-start | bytes 12582920 | tf_op jit(solution)/shard_map/while/body/eval_jaxpr/ppermute | solution.py:85
  2219.3 90.4 %collective-permute-start.1 = (bf16[1024,8,256]{2,0,1:T(8,128)(2,1)}, bf16[1024,8,256]{2,0,1:T(8,128)(2,1)}, u32[]{:S(2)}, u32[]{:S(2)}) collective-permute-start(bf16[1024,8,256]{2,0,1:T(8,128)(2,1)} %get-tuple-element.504), channel_id=1, source_target_pairs={{0,1},{1,2},{2,3},{3,4},{4,5},{5,6},{6,7},{7,0},{8,9},{9,10},{10,1... | collective-permute-start | bytes 12582920 | tf_op jit(solution)/shard_map/while/body/eval_jaxpr/ppermute | solution.py:85
  2334.3 47.9 %collective-permute-start = (bf16[1024,8,256]{2,0,1:T(8,128)(2,1)}, bf16[1024,8,256]{2,0,1:T(8,128)(2,1)}, u32[]{:S(2)}, u32[]{:S(2)}) collective-permute-start(bf16[1024,8,256]{2,0,1:T(8,128)(2,1)} %get-tuple-element.503), channel_id=1, source_target_pairs={{0,1},{1,2},{2,3},{3,4},{4,5},{5,6},{6,7},{7,0},{8,9},{9,10},{10,1... | collective-permute-start | bytes 12582920 | tf_op jit(solution)/shard_map/while/body/eval_jaxpr/ppermute | solution.py:85
  2336.8 90.4 %collective-permute-start.1 = (bf16[1024,8,256]{2,0,1:T(8,128)(2,1)}, bf16[1024,8,256]{2,0,1:T(8,128)(2,1)}, u32[]{:S(2)}, u32[]{:S(2)}) collective-permute-start(bf16[1024,8,256]{2,0,1:T(8,128)(2,1)} %get-tuple-element.504), channel_id=1, source_target_pairs={{0,1},{1,2},{2,3},{3,4},{4,5},{5,6},{6,7},{7,0},{8,9},{9,10},{10,1... | collective-permute-start | bytes 12582920 | tf_op jit(solution)/shard_map/while/body/eval_jaxpr/ppermute | solution.py:85
  2451.7 47.9 %collective-permute-start = (bf16[1024,8,256]{2,0,1:T(8,128)(2,1)}, bf16[1024,8,256]{2,0,1:T(8,128)(2,1)}, u32[]{:S(2)}, u32[]{:S(2)}) collective-permute-start(bf16[1024,8,256]{2,0,1:T(8,128)(2,1)} %get-tuple-element.503), channel_id=1, source_target_pairs={{0,1},{1,2},{2,3},{3,4},{4,5},{5,6},{6,7},{7,0},{8,9},{9,10},{10,1... | collective-permute-start | bytes 12582920 | tf_op jit(solution)/shard_map/while/body/eval_jaxpr/ppermute | solution.py:85
  2454.2 90.4 %collective-permute-start.1 = (bf16[1024,8,256]{2,0,1:T(8,128)(2,1)}, bf16[1024,8,256]{2,0,1:T(8,128)(2,1)}, u32[]{:S(2)}, u32[]{:S(2)}) collective-permute-start(bf16[1024,8,256]{2,0,1:T(8,128)(2,1)} %get-tuple-element.504), channel_id=1, source_target_pairs={{0,1},{1,2},{2,3},{3,4},{4,5},{5,6},{6,7},{7,0},{8,9},{9,10},{10,1... | collective-permute-start | bytes 12582920 | tf_op jit(solution)/shard_map/while/body/eval_jaxpr/ppermute | solution.py:85
  2569.2 47.9 %collective-permute-start = (bf16[1024,8,256]{2,0,1:T(8,128)(2,1)}, bf16[1024,8,256]{2,0,1:T(8,128)(2,1)}, u32[]{:S(2)}, u32[]{:S(2)}) collective-permute-start(bf16[1024,8,256]{2,0,1:T(8,128)(2,1)} %get-tuple-element.503), channel_id=1, source_target_pairs={{0,1},{1,2},{2,3},{3,4},{4,5},{5,6},{6,7},{7,0},{8,9},{9,10},{10,1... | collective-permute-start | bytes 12582920 | tf_op jit(solution)/shard_map/while/body/eval_jaxpr/ppermute | solution.py:85
  2571.7 90.4 %collective-permute-start.1 = (bf16[1024,8,256]{2,0,1:T(8,128)(2,1)}, bf16[1024,8,256]{2,0,1:T(8,128)(2,1)}, u32[]{:S(2)}, u32[]{:S(2)}) collective-permute-start(bf16[1024,8,256]{2,0,1:T(8,128)(2,1)} %get-tuple-element.504), channel_id=1, source_target_pairs={{0,1},{1,2},{2,3},{3,4},{4,5},{5,6},{6,7},{7,0},{8,9},{9,10},{10,1... | collective-permute-start | bytes 12582920 | tf_op jit(solution)/shard_map/while/body/eval_jaxpr/ppermute | solution.py:85
  2686.6 47.9 %collective-permute-start = (bf16[1024,8,256]{2,0,1:T(8,128)(2,1)}, bf16[1024,8,256]{2,0,1:T(8,128)(2,1)}, u32[]{:S(2)}, u32[]{:S(2)}) collective-permute-start(bf16[1024,8,256]{2,0,1:T(8,128)(2,1)} %get-tuple-element.503), channel_id=1, source_target_pairs={{0,1},{1,2},{2,3},{3,4},{4,5},{5,6},{6,7},{7,0},{8,9},{9,10},{10,1... | collective-permute-start | bytes 12582920 | tf_op jit(solution)/shard_map/while/body/eval_jaxpr/ppermute | solution.py:85
  2689.1 90.4 %collective-permute-start.1 = (bf16[1024,8,256]{2,0,1:T(8,128)(2,1)}, bf16[1024,8,256]{2,0,1:T(8,128)(2,1)}, u32[]{:S(2)}, u32[]{:S(2)}) collective-permute-start(bf16[1024,8,256]{2,0,1:T(8,128)(2,1)} %get-tuple-element.504), channel_id=1, source_target_pairs={{0,1},{1,2},{2,3},{3,4},{4,5},{5,6},{6,7},{7,0},{8,9},{9,10},{10,1... | collective-permute-start | bytes 12582920 | tf_op jit(solution)/shard_map/while/body/eval_jaxpr/ppermute | solution.py:85
  (87 other events, 1580.1 us)
where the time goes:
time: 2850 us; the launch traced here: 2830 us
  matrix products  1060 us (37%)
  local copies, waits for them, and re-layouts  610 us (21%)
  waiting for transfers between devices  609 us (21%)
  other arithmetic  499 us (18%)
  starting transfers between devices  50 us (2%)
    dot_general x18, matrix products, block_update(): jnp.einsum('...qhk,...khd->...qhd', prob_blk.astype(jnp.bfloat16), v_blk,...  381 us
    ppermute x14, waiting for transfers between devices, pass_step(): k_cur, v_cur = lax.ppermute((k_cur, v_cur), 'cp', next_pairs)  376 us
    dot_general x18, matrix products, block_update(): jnp.einsum('...qhd,...khd->...qhk', q_blk, k_blk, preferred_element_type=...  313 us
    reduce_sum x18, other arithmetic, block_update(): new_sum = run_sum * rescale + jnp.sum(prob_blk, axis=-1)  307 us
    dot_general x18, matrix products, project(): jnp.dot(normed, weight.reshape(d_model, n_heads * head_dim), preferred_el...  271 us
    unnamed x161, local copies, waits for them, and re-layouts  266 us
    ppermute x10, waiting for transfers between devices, device_body(): lax.ppermute((k_loc[n_tok - n_need:], v_loc[n_tok - n_need:]), 'cp', shif...  233 us
    reduce_max x5, other arithmetic, block_update(): new_max = jnp.maximum(run_max, jnp.max(scores, axis=-1))  176 us
  transfers between devices with their start and end apart: 24, of which 18 were waited for; matrix products, arithmetic and copies ran while one was open for 47% of the time, Pallas kernels for 0%

commit v1 on v0

v1 whole, which is shorter than its diff:
```python
import functools
import math

import jax
import jax.numpy as jnp
from jax import lax
from jax.experimental import pallas as pl
from jax.experimental.pallas import tpu as pltpu
from jax.sharding import PartitionSpec as P

WINDOW = 1024
NORM_EPS = 1e-6
NEG_BIG = -1e30
Q_ROWS = 256
G_ROWS = 512
N_COLS = 512
NORM_ROWS = 16
BF16 = jnp.bfloat16
F32 = jnp.float32
NT_DIMS = (((1,), (1,)), ((), ()))


def dot_nt(lhs, rhs):
    return lax.dot_general(lhs, rhs, NT_DIMS, preferred_element_type=F32)


def dot_nn(lhs, rhs):
    return jnp.dot(lhs, rhs, preferred_element_type=F32)


def aligned(start, size):
    return pl.ds(pl.multiple_of(start, size), size)


def norm_into(src_ref, src_row, dst_ref, dst_row, n_rows):
    def body(idx, carry):
        part = src_ref[pl.ds(pl.multiple_of(src_row + idx * NORM_ROWS, NORM_ROWS), NORM_ROWS), :].astype(F32)
        scale = lax.rsqrt(jnp.mean(part * part, axis=-1, keepdims=True) + NORM_EPS)
        dst_ref[pl.ds(pl.multiple_of(dst_row + idx * NORM_ROWS, NORM_ROWS), NORM_ROWS), :] = (part * scale).astype(BF16)
        return carry

    lax.fori_loop(0, n_rows // NORM_ROWS, body, 0, unroll=4)


def local_layers(n_cp, n_run, dims, x_hbm, wq_hbm, wk_hbm, wv_hbm, wo_hbm, out_hbm,
                 x_ref, halo, normed, qo, keys, vals, w_own, w_halo, w_out,
                 io_sem, own_sem, halo_sem, out_sem, send_sem, recv_sem, free_sem):
    n_tok, d_model, n_heads, head_dim = dims
    half = n_tok // 2
    n_cols = d_model // N_COLS
    exp_scale = head_dim ** -0.5 * math.log2(math.e)
    me = lax.axis_index("cp")
    right, left = lax.rem(me + 1, n_cp), lax.rem(me + n_cp - 1, n_cp)
    w_in = (wq_hbm, wk_hbm, wv_hbm)

    def own_copy(layer, head, slot, which):
        return pltpu.make_async_copy(w_in[which].at[layer, head], w_own.at[slot, which], own_sem.at[slot, which])

    def halo_copy(layer, head, slot, which):
        return pltpu.make_async_copy(w_in[which + 1].at[layer, head], w_halo.at[slot, which], halo_sem.at[slot, which])

    def out_copy(layer, col, slot):
        return pltpu.make_async_copy(wo_hbm.at[layer, :, aligned(col * N_COLS, N_COLS)], w_out.at[slot], out_sem.at[slot])

    def shift_copy(chunk):
        rows = pl.ds(pl.multiple_of((1 - chunk) * half, half), half)
        return pltpu.make_async_remote_copy(src_ref=x_ref.at[rows], dst_ref=halo.at[rows], send_sem=send_sem.at[chunk],
                                            recv_sem=recv_sem.at[chunk], device_id={"cp": right},
                                            device_id_type=pl.DeviceIdType.MESH)

    barrier = pltpu.get_barrier_semaphore()
    for neighbour in (left, right):
        pl.semaphore_signal(barrier, inc=1, device_id={"cp": neighbour}, device_id_type=pl.DeviceIdType.MESH)
    load = pltpu.make_async_copy(x_hbm, x_ref, io_sem)
    load.start()
    for which in range(3):
        own_copy(0, 0, 0, which).start()
    load.wait()
    pl.semaphore_wait(barrier, 2)
    for chunk in range(2):
        shift_copy(chunk).start()

    row_id = lax.broadcasted_iota(jnp.int32, (Q_ROWS, Q_ROWS), 0)
    col_id = lax.broadcasted_iota(jnp.int32, (Q_ROWS, Q_ROWS), 1)

    def attend(q_blk, cols):
        q_rows = aligned(q_blk * Q_ROWS, Q_ROWS)
        k_rows = pl.ds(pl.multiple_of(q_blk * Q_ROWS, Q_ROWS), WINDOW + Q_ROWS)
        scores = dot_nt(qo[q_rows, cols], keys[k_rows, cols])
        n_blk = WINDOW // Q_ROWS
        parts = [scores[:, blk * Q_ROWS:(blk + 1) * Q_ROWS] for blk in range(n_blk + 1)]
        parts[0] = jnp.where(col_id > row_id, parts[0], NEG_BIG)
        parts[n_blk] = jnp.where(col_id <= row_id, parts[n_blk], NEG_BIG)
        for blk in range(n_blk):
            parts[blk] = jnp.where((me > 0) | (q_blk + blk >= n_blk), parts[blk], NEG_BIG)
        top = functools.reduce(jnp.maximum, parts)
        top = jnp.max(top, axis=-1, keepdims=True)
        probs = [jnp.exp2((part - top) * exp_scale) for part in parts]
        total = jnp.sum(functools.reduce(jnp.add, probs), axis=-1, keepdims=True)
        weights = jnp.concatenate([prob.astype(BF16) for prob in probs], axis=1)
        qo[q_rows, cols] = (dot_nn(weights, vals[k_rows, cols]) / total).astype(BF16)

    def layer_step(layer, carry):
        norm_into(x_ref, 0, normed, 0, n_tok)
        for which in range(2):
            halo_copy(layer, 0, 0, which).start()

        def own_step(head, inner):
            slot = lax.rem(head, 2)

            @pl.when(head + 1 < n_heads)
            def _():
                for which in range(3):
                    own_copy(layer, head + 1, 1 - slot, which).start()

            cols = aligned(head * head_dim, head_dim)
            for which, (dst, base) in enumerate(((qo, 0), (keys, n_tok), (vals, n_tok))):
                own_copy(layer, head, slot, which).wait()
                for part in range(2):
                    dst[pl.ds(base + part * half, half), cols] = dot_nn(
                        normed[pl.ds(part * half, half), :], w_own[slot, which]).astype(BF16)
            return inner

        lax.fori_loop(0, n_heads, own_step, 0)

        def chunk_step(chunk, inner):
            row0 = pl.multiple_of((1 - chunk) * half, half)
            rows = pl.ds(row0, half)
            shift_copy(chunk).wait_recv()
            norm_into(halo, row0, normed, 0, half)

            @pl.when(layer + 1 < n_run)
            def _():
                pl.semaphore_signal(free_sem.at[chunk], inc=1, device_id={"cp": left}, device_id_type=pl.DeviceIdType.MESH)

            out_copy(layer, 0, 0).start()

            def head_step(head, deep):
                slot = lax.rem(head, 2)

                @pl.when(head + 1 < n_heads)
                def _():
                    for which in range(2):
                        halo_copy(layer, head + 1, 1 - slot, which).start()

                @pl.when((head + 1 == n_heads) & (chunk == 0))
                def _():
                    for which in range(2):
                        halo_copy(layer, 0, 1 - slot, which).start()

                @pl.when((head + 1 == n_heads) & (chunk == 1) & (layer + 1 < n_run))
                def _():
                    for which in range(3):
                        own_copy(layer + 1, 0, 0, which).start()

                cols = aligned(head * head_dim, head_dim)
                for which, dst in enumerate((keys, vals)):
                    halo_copy(layer, head, slot, which).wait()
                    dst[rows, cols] = dot_nn(normed[pl.ds(0, half), :], w_halo[slot, which]).astype(BF16)
                for sub in range(half // Q_ROWS):
                    attend((1 - chunk) * (half // Q_ROWS) + sub, cols)
                return deep

            lax.fori_loop(0, n_heads, head_step, 0)
            shift_copy(chunk).wait_send()

            def col_step(col, deep):
                slot = lax.rem(col, 2)

                @pl.when(col + 1 < n_cols)
                def _():
                    out_copy(layer, col + 1, 1 - slot).start()

                out_copy(layer, col, slot).wait()
                cols = aligned(col * N_COLS, N_COLS)
                x_ref[rows, cols] = (x_ref[rows, cols].astype(F32) + dot_nn(qo[rows, :], w_out[slot])).astype(BF16)
                return deep

            lax.fori_loop(0, n_cols, col_step, 0)

            @pl.when(layer + 1 < n_run)
            def _():
                pl.semaphore_wait(free_sem.at[chunk], 1)
                shift_copy(chunk).start()

            return inner

        lax.fori_loop(0, 2, chunk_step, 0)
        return carry

    lax.fori_loop(0, n_run, layer_step, 0)
    store = pltpu.make_async_copy(x_ref, out_hbm, io_sem)
    store.start()
    store.wait()


def global_layer(n_cp, layer, offsets, dims, x_hbm, wq_hbm, wk_hbm, wv_hbm, wo_hbm, out_hbm,
                 x_ref, normed, stage, held, o_stage, o_all, w_own, w_out, run_max, run_sum, acc,
                 io_sem, own_sem, out_sem, send_sem, recv_sem, o_send, o_recv):
    n_tok, d_model, n_heads, head_dim = dims
    half = n_tok // 2
    n_cols = d_model // N_COLS
    exp_scale = head_dim ** -0.5 * math.log2(math.e)
    me = lax.axis_index("cp")
    w_in = (wq_hbm, wk_hbm, wv_hbm)

    def peer(step):
        shift = jnp.int32(0)
        for idx, offset in enumerate(offsets):
            shift = jnp.where(step == idx, offset, shift)
        return lax.rem(me + shift, n_cp)

    def own_copy(head, slot, which):
        return pltpu.make_async_copy(w_in[which].at[layer, head], w_own.at[slot, which], own_sem.at[slot, which])

    def out_copy(col, slot):
        return pltpu.make_async_copy(wo_hbm.at[layer, :, aligned(col * N_COLS, N_COLS)], w_out.at[slot], out_sem.at[slot])

    def give_copy(dst):
        return pltpu.make_async_remote_copy(src_ref=stage.at[dst], dst_ref=held.at[me], send_sem=send_sem.at[dst],
                                            recv_sem=recv_sem.at[me], device_id={"cp": dst},
                                            device_id_type=pl.DeviceIdType.MESH)

    def take_wait(src):
        pltpu.make_async_remote_copy(src_ref=held.at[src], dst_ref=held.at[src], send_sem=send_sem.at[src],
                                     recv_sem=recv_sem.at[src], device_id={"cp": src},
                                     device_id_type=pl.DeviceIdType.MESH).wait_recv()

    my_cols = aligned(me * head_dim, head_dim)

    def back_copy(dst):
        return pltpu.make_async_remote_copy(src_ref=o_stage.at[dst], dst_ref=o_all.at[:, my_cols], send_sem=o_send.at[dst],
                                            recv_sem=o_recv.at[me], device_id={"cp": dst},
                                            device_id_type=pl.DeviceIdType.MESH)

    def back_wait(src):
        pltpu.make_async_remote_copy(src_ref=o_stage.at[src], dst_ref=o_all.at[:, aligned(src * head_dim, head_dim)],
                                     send_sem=o_send.at[src], recv_sem=o_recv.at[src], device_id={"cp": src},
                                     device_id_type=pl.DeviceIdType.MESH).wait_recv()

    barrier = pltpu.get_barrier_semaphore()
    for shift in range(1, n_cp):
        pl.semaphore_signal(barrier, inc=1, device_id={"cp": lax.rem(me + shift, n_cp)}, device_id_type=pl.DeviceIdType.MESH)
    load = pltpu.make_async_copy(x_hbm, x_ref, io_sem)
    load.start()
    for which in range(3):
        own_copy(peer(0), 0, which).start()
    load.wait()
    norm_into(x_ref, 0, normed, 0, n_tok)
    pl.semaphore_wait(barrier, n_cp - 1)

    def own_step(step, carry):
        slot = lax.rem(step, 2)
        head = peer(step)

        @pl.when(step + 1 < n_heads)
        def _():
            for which in range(3):
                own_copy(peer(step + 1), 1 - slot, which).start()

        for which in range(3):
            own_copy(head, slot, which).wait()
            for part in range(2):
                stage[head, which, pl.ds(part * half, half), :] = dot_nn(
                    normed[pl.ds(part * half, half), :], w_own[slot, which]).astype(BF16)

        @pl.when(step + 1 < n_heads)
        def _():
            give_copy(head).start()

        return carry

    lax.fori_loop(0, n_heads, own_step, 0)

    def keep_step(idx, carry):
        rows = aligned(idx * 128, 128)
        for which in range(3):
            held[me, which, rows, :] = stage[me, which, rows, :]
        return carry

    lax.fori_loop(0, n_tok // 128, keep_step, 0)
    out_copy(0, 0).start()

    row_id = lax.broadcasted_iota(jnp.int32, (G_ROWS, G_ROWS), 0)
    col_id = lax.broadcasted_iota(jnp.int32, (G_ROWS, G_ROWS), 1)
    per_src = n_tok // G_ROWS

    def block_update(q_src, q_rows, k_src, k_rows, masked):
        scores = dot_nt(held[q_src, 0, q_rows, :], held[k_src, 1, k_rows, :])
        if masked:
            scores = jnp.where(col_id <= row_id, scores, NEG_BIG)
        old_max = run_max[:, :1]
        new_max = jnp.maximum(old_max, jnp.max(scores, axis=-1, keepdims=True))
        probs = jnp.exp2((scores - new_max) * exp_scale)
        rescale = jnp.exp2((old_max - new_max) * exp_scale)
        new_sum = run_sum[:, :1] * rescale + jnp.sum(probs, axis=-1, keepdims=True)
        run_sum[...] = jnp.broadcast_to(new_sum, run_sum.shape)
        run_max[...] = jnp.broadcast_to(new_max, run_max.shape)
        acc[...] = acc[...] * rescale + dot_nn(probs.astype(BF16), held[k_src, 2, k_rows, :])

    def src_step(src, carry):
        @pl.when(src != me)
        def _():
            take_wait(src)

        def row_step(sub, inner):
            q_rows = aligned(sub * G_ROWS, G_ROWS)
            run_max[...] = jnp.full(run_max.shape, NEG_BIG, F32)
            run_sum[...] = jnp.zeros(run_sum.shape, F32)
            acc[...] = jnp.zeros(acc.shape, F32)

            def key_step(key, deep):
                block_update(src, q_rows, key // per_src, aligned(lax.rem(key, per_src) * G_ROWS, G_ROWS), False)
                return deep

            lax.fori_loop(0, src * per_src + sub, key_step, 0)
            block_update(src, q_rows, src, q_rows, True)
            o_stage[src, q_rows, :] = (acc[...] / run_sum[:, :1]).astype(BF16)
            return inner

        lax.fori_loop(0, per_src, row_step, 0)

        @pl.when(src != me)
        def _():
            back_copy(src).start()

        @pl.when(src == me)
        def _():
            o_all[:, my_cols] = o_stage[src]

        return carry

    lax.fori_loop(0, n_cp, src_step, 0)

    def done_step(src, carry):
        @pl.when(src != me)
        def _():
            give_copy(src).wait_send()
            back_copy(src).wait_send()
            back_wait(src)

        return carry

    lax.fori_loop(0, n_cp, done_step, 0)

    def col_step(col, carry):
        slot = lax.rem(col, 2)

        @pl.when(col + 1 < n_cols)
        def _():
            out_copy(col + 1, 1 - slot).start()

        out_copy(col, slot).wait()
        cols = aligned(col * N_COLS, N_COLS)
        for part in range(2):
            rows = pl.ds(part * half, half)
            x_ref[rows, cols] = (x_ref[rows, cols].astype(F32) + dot_nn(o_all[rows, :], w_out[slot])).astype(BF16)
        return carry

    lax.fori_loop(0, n_cols, col_step, 0)
    store = pltpu.make_async_copy(x_ref, out_hbm, io_sem)
    store.start()
    store.wait()


def solution(mesh):
    n_cp = mesh.shape["cp"]

    def device_body(hidden, w_query, w_key, w_value, w_out):
        n_tok, d_model = hidden.shape
        n_layers, _, n_heads, head_dim = w_query.shape
        width = n_heads * head_dim
        dims = (n_tok, d_model, n_heads, head_dim)
        assert n_tok == WINDOW and n_heads == n_cp
        w_heads = [jnp.transpose(w, (0, 2, 1, 3)) for w in (w_query, w_key, w_value)]
        w_flat = w_out.reshape(n_layers, width, d_model)
        any_spec = pl.BlockSpec(memory_space=pl.ANY)
        dma = pltpu.SemaphoreType.DMA
        vmem = pltpu.VMEM
        big = 60 * 1024 * 1024
        flops = 2 * n_tok * d_model * width
        hidden = pl.pallas_call(
            functools.partial(local_layers, n_cp, n_layers - 1, dims),
            out_shape=jax.ShapeDtypeStruct(hidden.shape, hidden.dtype),
            in_specs=[any_spec] * 5, out_specs=any_spec,
            scratch_shapes=[
                vmem((n_tok, d_model), BF16), vmem((n_tok, d_model), BF16), vmem((n_tok, d_model), BF16),
                vmem((n_tok, width), BF16), vmem((2 * n_tok, width), BF16), vmem((2 * n_tok, width), BF16),
                vmem((2, 3, d_model, head_dim), BF16), vmem((2, 2, d_model, head_dim), BF16), vmem((2, width, N_COLS), BF16),
                dma, dma((2, 3)), dma((2, 2)), dma((2,)), dma((2,)), dma((2,)), pltpu.SemaphoreType.REGULAR((2,)),
            ],
            compiler_params=pltpu.CompilerParams(collective_id=0, has_side_effects=True, vmem_limit_bytes=big),
            cost_estimate=pl.CostEstimate(flops=5 * 7 * flops, bytes_accessed=5 * 63 * 2 ** 20, transcendentals=0),
            name="local_layers",
        )(hidden, *w_heads, w_flat)
        order = sorted(range(1, n_cp), key=lambda off: (-min(off, n_cp - off), off)) + [0]
        return pl.pallas_call(
            functools.partial(global_layer, n_cp, n_layers - 1, order, dims),
            out_shape=jax.ShapeDtypeStruct(hidden.shape, hidden.dtype),
            in_specs=[any_spec] * 5, out_specs=any_spec,
            scratch_shapes=[
                vmem((n_tok, d_model), BF16), vmem((n_tok, d_model), BF16),
                vmem((n_heads, 3, n_tok, head_dim), BF16), vmem((n_cp, 3, n_tok, head_dim), BF16),
                vmem((n_cp, n_tok, head_dim), BF16), vmem((n_tok, width), BF16),
                vmem((2, 3, d_model, head_dim), BF16), vmem((2, width, N_COLS), BF16),
                vmem((G_ROWS, 128), F32), vmem((G_ROWS, 128), F32), vmem((G_ROWS, head_dim), F32),
                dma, dma((2, 3)), dma((2,)), dma((n_cp,)), dma((n_cp,)), dma((n_cp,)), dma((n_cp,)),
            ],
            compiler_params=pltpu.CompilerParams(collective_id=1, has_side_effects=True, vmem_limit_bytes=big),
            cost_estimate=pl.CostEstimate(flops=8 * flops, bytes_accessed=63 * 2 ** 20, transcendentals=0),
            name="global_layer",
        )(hidden, *w_heads, w_flat)

    row_spec = P(("dp", "cp"), None)
    return jax.shard_map(device_body, mesh=mesh, in_specs=(row_spec, P(), P(), P(), P()), out_specs=row_spec, check_vma=False)
```

time: 2850 us -> 1200 us (0.42)
  matrix products: 1060 us -> 0 us
  Pallas kernels: 0 us -> 1050 us
  waiting for transfers between devices: 609 us -> 0 us
  other arithmetic: 499 us -> 0 us
  local copies, waits for them, and re-layouts: 610 us -> 129 us
  starting transfers between devices: 50 us -> 0 us
    dot_general x60 -> x0, matrix products: 1060 us -> none  [the longest x18 381 us: block_update(): jnp.einsum('...qhk,...khd->...qhd', prob_blk.astype(jnp.bfloat16), v_blk,...]
    pallas_call x0 -> x2, Pallas kernels: none -> 1050 us  [the longest x1 662 us: device_body(): pl.pallas_call(functools.partial(local_layers, n_cp, n_layers - 1, dims),...]
    ppermute x24 -> x0, waiting for transfers between devices: 609 us -> none  [the longest x14 376 us: pass_step(): k_cur, v_cur = lax.ppermute((k_cur, v_cur), 'cp', next_pairs)]
    reduce_sum x19 -> x0, other arithmetic: 310 us -> none  [the longest x18 307 us: block_update(): new_sum = run_sum * rescale + jnp.sum(prob_blk, axis=-1)]
    unnamed x161 -> x2, local copies, waits for them, and re-layouts: 266 us -> 46.6 us
    slice x24 -> x0, local copies, waits for them, and re-layouts: 209 us -> none  [the longest x1 42 us: device_body(): hidden = out_update(hidden, finish(soft_state), w_out[layer_idx])]
    reduce_max x5 -> x0, other arithmetic: 176 us -> none  [block_update(): new_max = jnp.maximum(run_max, jnp.max(scores, axis=-1))]
    while x64 -> x0, local copies, waits for them, and re-layouts: 96.5 us -> none
  transfers between devices with their start and end apart: 24 -> 0, of which waited for: 18 -> 0; matrix products, arithmetic and copies ran while one was open for 47% -> 0% of each run, Pallas kernels for 0% -> 0%
where the time goes in v1:
time: 1200 us; the launch traced here: 1180 us
  Pallas kernels  1050 us (88%)
  local copies, waits for them, and re-layouts  129 us (11%)
    pallas_call x1, Pallas kernels, device_body(): pl.pallas_call(functools.partial(local_layers, n_cp, n_layers - 1, dims),...  662 us
    pallas_call x1, Pallas kernels, device_body(): pl.pallas_call(functools.partial(global_layer, n_cp, n_layers - 1, order,...  391 us
    transpose x1, local copies, waits for them, and re-layouts, device_body(): jnp.transpose(w, (0, 2, 1, 3))  82.1 us
    unnamed x2, local copies, waits for them, and re-layouts  46.6 us

profile of v1, /device:TPU:113, one launch (start us, length us, event | category | flops | bytes accessed | tf_op | source)
XLA Modules:
  0.0 1181.8 jit_solution(10595022113313263961)
XLA Ops:
  0.0 41.5 %copy.12 = bf16[6,2560,8,256]{3,1,2,0:T(8,128)(2,1)} copy(bf16[6,2560,8,256]{3,2,1,0:T(8,128)(2,1)} %param.6) | data formatting | bytes 125829120 | tf_op args[1]
  41.5 82.1 %copy_bitcast_fusion = (bf16[6,8,2560,256]{3,2,1,0:T(8,128)(2,1)}, bf16[6,8,2560,256]{3,2,1,0:T(8,128)(2,1)}) fusion(bf16[6,2560,8,256]{3,2,1,0:T(8,128)(2,1)} %param.8, bf16[6,2560,8,256]{3,2,1,0:T(8,128)(2,1)} %param.7), kind=kLoop, calls=%fused_computation | loop fusion | bytes 251658240 | tf_op jit(solution)/shard_map/transpose | solution.py:375
  123.6 662.2 %local_layers.1.x_hbm = bf16[1024,2560]{1,0:T(8,128)(2,1)} custom-call(bf16[1024,2560]{1,0:T(8,128)(2,1)} %x_hbm.1, bf16[6,8,2560,256]{3,2,1,0:T(8,128)(2,1)} %bitcast.8, bf16[6,8,2560,256]{3,2,1,0:T(8,128)(2,1)} %get-tuple-element.6.wk_hbm, bf16[6,8,2560,256]{3,2,1,0:T(8,128)(2,1)} %get-tuple-element.5.wv_hbm, bf16[6,2048,2560]{2,1,0:T(8,128)(2,1)} %bitcast.10), custom_call_target="tpu_custom_call" | custom-call | flops 375809638400 | bytes 330301440 | tf_op jit(solution)/shard_map/local_layers/pallas_call | solution.py:382
  785.8 390.9 %global_layer.1 = bf16[1024,2560]{1,0:T(8,128)(2,1)} custom-call(bf16[1024,2560]{1,0:T(8,128)(2,1)} %local_layers.1.x_hbm, bf16[6,8,2560,256]{3,2,1,0:T(8,128)(2,1)} %bitcast.9, bf16[6,8,2560,256]{3,2,1,0:T(8,128)(2,1)} %get-tuple-element.6.wk_hbm, bf16[6,8,2560,256]{3,2,1,0:T(8,128)(2,1)} %get-tuple-element.5.wv_hbm, bf16[6,2048,2560]{2,1,0:T(8,128)(2,1)} %bitcast.11), custom_call_target="tpu_custom_call" | custom-call | flops 85899345920 | bytes 66060288 | tf_op jit(solution)/shard_map/global_layer/pallas_call | solution.py:397
  1176.6 5.2 copy.14

commit v2 on v1

--- a/solution.py
+++ b/solution.py
@@ -12,7 +12,6 @@
 NORM_EPS = 1e-6
 NEG_BIG = -1e30
 Q_ROWS = 256
-G_ROWS = 512
 N_COLS = 512
 NORM_ROWS = 16
 BF16 = jnp.bfloat16
@@ -43,7 +42,7 @@
 
 
 def local_layers(n_cp, n_run, dims, x_hbm, wq_hbm, wk_hbm, wv_hbm, wo_hbm, out_hbm,
-                 x_ref, halo, normed, qo, keys, vals, w_own, w_halo, w_out,
+                 x_ref, halo, normed, qo, keys, vals, k_next, v_next, w_own, w_halo, w_out,
                  io_sem, own_sem, halo_sem, out_sem, send_sem, recv_sem, free_sem):
     n_tok, d_model, n_heads, head_dim = dims
     half = n_tok // 2
@@ -83,11 +82,14 @@
     row_id = lax.broadcasted_iota(jnp.int32, (Q_ROWS, Q_ROWS), 0)
     col_id = lax.broadcasted_iota(jnp.int32, (Q_ROWS, Q_ROWS), 1)
 
-    def attend(q_blk, cols):
-        q_rows = aligned(q_blk * Q_ROWS, Q_ROWS)
-        k_rows = pl.ds(pl.multiple_of(q_blk * Q_ROWS, Q_ROWS), WINDOW + Q_ROWS)
-        scores = dot_nt(qo[q_rows, cols], keys[k_rows, cols])
-        n_blk = WINDOW // Q_ROWS
+    n_sub = half // Q_ROWS
+    n_blk = WINDOW // Q_ROWS
+
+    def project_halo(slot, which):
+        dst = (k_next, v_next)[which]
+        dst[...] = dot_nn(normed[pl.ds(0, half), :], w_halo[slot, which]).astype(BF16)
+
+    def soften(scores, q_blk):
         parts = [scores[:, blk * Q_ROWS:(blk + 1) * Q_ROWS] for blk in range(n_blk + 1)]
         parts[0] = jnp.where(col_id > row_id, parts[0], NEG_BIG)
         parts[n_blk] = jnp.where(col_id <= row_id, parts[n_blk], NEG_BIG)
@@ -97,13 +99,25 @@
         top = jnp.max(top, axis=-1, keepdims=True)
         probs = [jnp.exp2((part - top) * exp_scale) for part in parts]
         total = jnp.sum(functools.reduce(jnp.add, probs), axis=-1, keepdims=True)
-        weights = jnp.concatenate([prob.astype(BF16) for prob in probs], axis=1)
-        qo[q_rows, cols] = (dot_nn(weights, vals[k_rows, cols]) / total).astype(BF16)
+        return jnp.concatenate([prob.astype(BF16) for prob in probs], axis=1), total
+
+    def attend(chunk, cols, side_k, side_v):
+        blks = [(1 - chunk) * n_sub + sub for sub in range(n_sub)]
+        q_rows = [aligned(blk * Q_ROWS, Q_ROWS) for blk in blks]
+        k_rows = [pl.ds(pl.multiple_of(blk * Q_ROWS, Q_ROWS), WINDOW + Q_ROWS) for blk in blks]
+        scores = [dot_nt(qo[q_rows[sub], cols], keys[k_rows[sub], cols]) for sub in range(n_sub)]
+        side_k()
+        soft = [soften(scores[sub], blks[sub]) for sub in range(n_sub)]
+        side_v()
+        outs = [dot_nn(soft[sub][0], vals[k_rows[sub], cols]) / soft[sub][1] for sub in range(n_sub)]
+        for sub in range(n_sub):
+            qo[q_rows[sub], cols] = outs[sub].astype(BF16)
 
     def layer_step(layer, carry):
         norm_into(x_ref, 0, normed, 0, n_tok)
-        for which in range(2):
-            halo_copy(layer, 0, 0, which).start()
+        for head in range(2):
+            for which in range(2):
+                halo_copy(layer, head, head, which).start()
 
         def own_step(head, inner):
             slot = lax.rem(head, 2)
@@ -135,33 +149,49 @@
 
             out_copy(layer, 0, 0).start()
 
+            def keep(cols):
+                keys[rows, cols] = k_next[...]
+                vals[rows, cols] = v_next[...]
+
+            for which in range(2):
+                halo_copy(layer, 0, 0, which).wait()
+                project_halo(0, which)
+
             def head_step(head, deep):
                 slot = lax.rem(head, 2)
 
-                @pl.when(head + 1 < n_heads)
+                @pl.when(head + 2 < n_heads)
                 def _():
                     for which in range(2):
-                        halo_copy(layer, head + 1, 1 - slot, which).start()
-
-                @pl.when((head + 1 == n_heads) & (chunk == 0))
+                        halo_copy(layer, head + 2, slot, which).start()
+
+                @pl.when((head + 2 == n_heads) & (chunk == 0))
                 def _():
                     for which in range(2):
-                        halo_copy(layer, 0, 1 - slot, which).start()
-
-                @pl.when((head + 1 == n_heads) & (chunk == 1) & (layer + 1 < n_run))
+                        halo_copy(layer, 0, slot, which).start()
+
+                @pl.when((head + 2 == n_heads) & (chunk == 1) & (layer + 1 < n_run))
                 def _():
                     for which in range(3):
                         own_copy(layer + 1, 0, 0, which).start()
 
+                for which in range(2):
+                    halo_copy(layer, head + 1, 1 - slot, which).wait()
                 cols = aligned(head * head_dim, head_dim)
-                for which, dst in enumerate((keys, vals)):
-                    halo_copy(layer, head, slot, which).wait()
-                    dst[rows, cols] = dot_nn(normed[pl.ds(0, half), :], w_halo[slot, which]).astype(BF16)
-                for sub in range(half // Q_ROWS):
-                    attend((1 - chunk) * (half // Q_ROWS) + sub, cols)
+                keep(cols)
+                attend(chunk, cols, lambda: project_halo(1 - slot, 0), lambda: project_halo(1 - slot, 1))
                 return deep
 
-            lax.fori_loop(0, n_heads, head_step, 0)
+            lax.fori_loop(0, n_heads - 1, head_step, 0)
+
+            @pl.when(chunk == 0)
+            def _():
+                for which in range(2):
+                    halo_copy(layer, 1, 1, which).start()
+
+            last = pl.ds((n_heads - 1) * head_dim, head_dim)
+            keep(last)
+            attend(chunk, last, lambda: None, lambda: None)
             shift_copy(chunk).wait_send()
 
             def col_step(col, deep):
@@ -194,21 +224,31 @@
     store.wait()
 
 
-def global_layer(n_cp, layer, offsets, dims, x_hbm, wq_hbm, wk_hbm, wv_hbm, wo_hbm, out_hbm,
-                 x_ref, normed, stage, held, o_stage, o_all, w_own, w_out, run_max, run_sum, acc,
-                 io_sem, own_sem, out_sem, send_sem, recv_sem, o_send, o_recv):
+def global_layer(n_cp, layer, dims, x_hbm, wq_hbm, wk_hbm, wv_hbm, wo_hbm, out_hbm,
+                 x_ref, stage, held, relay, o_stage, o_all, w_own, w_out, *rest):
     n_tok, d_model, n_heads, head_dim = dims
     half = n_tok // 2
     n_cols = d_model // N_COLS
     exp_scale = head_dim ** -0.5 * math.log2(math.e)
+    n_grp = n_tok // Q_ROWS
+    run_max, run_sum, acc = rest[:n_grp], rest[n_grp:2 * n_grp], rest[2 * n_grp:3 * n_grp]
+    io_sem, own_sem, out_sem, send_sem, recv_sem, o_send, o_recv, relay_send, relay_recv = rest[3 * n_grp:]
     me = lax.axis_index("cp")
     w_in = (wq_hbm, wk_hbm, wv_hbm)
+    mate = me + 1 - 2 * lax.rem(me, 2)
+    far, back = n_cp // 2, n_cp - 2
+    via = lax.rem(me + back, n_cp)
+    relay_dst = lax.rem(mate + far, n_cp)
+    relay_src = lax.rem(me + 2, n_cp)
+    relay_end = lax.rem(mate + back, n_cp)
+    peers = [relay_dst, lax.rem(me + far, n_cp), lax.rem(me + 2, n_cp), lax.rem(me + back, n_cp),
+             lax.rem(mate + 2, n_cp), lax.rem(mate + back, n_cp), mate, me]
 
     def peer(step):
-        shift = jnp.int32(0)
-        for idx, offset in enumerate(offsets):
-            shift = jnp.where(step == idx, offset, shift)
-        return lax.rem(me + shift, n_cp)
+        head = me
+        for idx, other in enumerate(peers):
+            head = jnp.where(step == idx, other, head)
+        return head
 
     def own_copy(head, slot, which):
         return pltpu.make_async_copy(w_in[which].at[layer, head], w_own.at[slot, which], own_sem.at[slot, which])
@@ -219,6 +259,16 @@
     def give_copy(dst):
         return pltpu.make_async_remote_copy(src_ref=stage.at[dst], dst_ref=held.at[me], send_sem=send_sem.at[dst],
                                             recv_sem=recv_sem.at[me], device_id={"cp": dst},
+                                            device_id_type=pl.DeviceIdType.MESH)
+
+    def relay_copy():
+        return pltpu.make_async_remote_copy(src_ref=stage.at[relay_dst], dst_ref=relay, send_sem=send_sem.at[relay_dst],
+                                            recv_sem=relay_recv, device_id={"cp": via},
+                                            device_id_type=pl.DeviceIdType.MESH)
+
+    def forward_copy():
+        return pltpu.make_async_remote_copy(src_ref=relay, dst_ref=held.at[relay_src], send_sem=relay_send,
+                                            recv_sem=recv_sem.at[relay_src], device_id={"cp": relay_end},
                                             device_id_type=pl.DeviceIdType.MESH)
 
     def take_wait(src):
@@ -246,7 +296,7 @@
     for which in range(3):
         own_copy(peer(0), 0, which).start()
     load.wait()
-    norm_into(x_ref, 0, normed, 0, n_tok)
+    norm_into(x_ref, 0, x_ref, 0, n_tok)
     pl.semaphore_wait(barrier, n_cp - 1)
 
     def own_step(step, carry):
@@ -262,15 +312,22 @@
             own_copy(head, slot, which).wait()
             for part in range(2):
                 stage[head, which, pl.ds(part * half, half), :] = dot_nn(
-                    normed[pl.ds(part * half, half), :], w_own[slot, which]).astype(BF16)
-
-        @pl.when(step + 1 < n_heads)
+                    x_ref[pl.ds(part * half, half), :], w_own[slot, which]).astype(BF16)
+
+        @pl.when(step == 0)
+        def _():
+            relay_copy().start()
+
+        @pl.when((step > 0) & (step + 1 < n_heads))
         def _():
             give_copy(head).start()
 
         return carry
 
     lax.fori_loop(0, n_heads, own_step, 0)
+    load.start()
+    relay_copy().wait_recv()
+    forward_copy().start()
 
     def keep_step(idx, carry):
         rows = aligned(idx * 128, 128)
@@ -281,44 +338,52 @@
     lax.fori_loop(0, n_tok // 128, keep_step, 0)
     out_copy(0, 0).start()
 
-    row_id = lax.broadcasted_iota(jnp.int32, (G_ROWS, G_ROWS), 0)
-    col_id = lax.broadcasted_iota(jnp.int32, (G_ROWS, G_ROWS), 1)
-    per_src = n_tok // G_ROWS
-
-    def block_update(q_src, q_rows, k_src, k_rows, masked):
-        scores = dot_nt(held[q_src, 0, q_rows, :], held[k_src, 1, k_rows, :])
-        if masked:
-            scores = jnp.where(col_id <= row_id, scores, NEG_BIG)
-        old_max = run_max[:, :1]
-        new_max = jnp.maximum(old_max, jnp.max(scores, axis=-1, keepdims=True))
+    row_id = lax.broadcasted_iota(jnp.int32, (Q_ROWS, Q_ROWS), 0)
+    col_id = lax.broadcasted_iota(jnp.int32, (Q_ROWS, Q_ROWS), 1)
+    grp_rows = [pl.ds(grp * Q_ROWS, Q_ROWS) for grp in range(n_grp)]
+
+    def score(q_src, k_src, grp, n_key):
+        return dot_nt(held[q_src, 0, grp_rows[grp], :], held[k_src, 1, pl.ds(0, n_key), :])
+
+    def update(grp, scores, k_src, n_key, first):
+        new_max = jnp.max(scores, axis=-1, keepdims=True)
+        if not first:
+            old_max = run_max[grp][:, :1]
+            new_max = jnp.maximum(old_max, new_max)
         probs = jnp.exp2((scores - new_max) * exp_scale)
-        rescale = jnp.exp2((old_max - new_max) * exp_scale)
-        new_sum = run_sum[:, :1] * rescale + jnp.sum(probs, axis=-1, keepdims=True)
-        run_sum[...] = jnp.broadcast_to(new_sum, run_sum.shape)
-        run_max[...] = jnp.broadcast_to(new_max, run_max.shape)
-        acc[...] = acc[...] * rescale + dot_nn(probs.astype(BF16), held[k_src, 2, k_rows, :])
+        new_sum = jnp.sum(probs, axis=-1, keepdims=True)
+        if not first:
+            rescale = jnp.exp2((old_max - new_max) * exp_scale)
+            new_sum = run_sum[grp][:, :1] * rescale + new_sum
+        run_sum[grp][...] = jnp.broadcast_to(new_sum, run_sum[grp].shape)
+        run_max[grp][...] = jnp.broadcast_to(new_max, run_max[grp].shape)
+        new_acc = dot_nn(probs.astype(BF16), held[k_src, 2, pl.ds(0, n_key), :])
+        acc[grp][...] = new_acc if first else acc[grp][...] * rescale + new_acc
 
     def src_step(src, carry):
         @pl.when(src != me)
         def _():
             take_wait(src)
 
-        def row_step(sub, inner):
-            q_rows = aligned(sub * G_ROWS, G_ROWS)
-            run_max[...] = jnp.full(run_max.shape, NEG_BIG, F32)
-            run_sum[...] = jnp.zeros(run_sum.shape, F32)
-            acc[...] = jnp.zeros(acc.shape, F32)
-
-            def key_step(key, deep):
-                block_update(src, q_rows, key // per_src, aligned(lax.rem(key, per_src) * G_ROWS, G_ROWS), False)
-                return deep
-
-            lax.fori_loop(0, src * per_src + sub, key_step, 0)
-            block_update(src, q_rows, src, q_rows, True)
-            o_stage[src, q_rows, :] = (acc[...] / run_sum[:, :1]).astype(BF16)
+        scores = []
+        for grp in range(n_grp):
+            full = score(src, src, grp, (grp + 1) * Q_ROWS)
+            diag = jnp.where(col_id <= row_id, full[:, grp * Q_ROWS:], NEG_BIG)
+            scores.append(jnp.concatenate([full[:, :grp * Q_ROWS], diag], axis=1) if grp else diag)
+        for grp in range(n_grp):
+            update(grp, scores[grp], src, (grp + 1) * Q_ROWS, True)
+
+        def key_step(k_src, inner):
+            ready = [score(src, k_src, 0, n_tok)]
+            for grp in range(n_grp):
+                if grp + 1 < n_grp:
+                    ready.append(score(src, k_src, grp + 1, n_tok))
+                update(grp, ready[grp], k_src, n_tok, False)
             return inner
 
-        lax.fori_loop(0, per_src, row_step, 0)
+        lax.fori_loop(0, src, key_step, 0)
+        for grp in range(n_grp):
+            o_stage[src, grp_rows[grp], :] = (acc[grp][...] / run_sum[grp][:, :1]).astype(BF16)
 
         @pl.when(src != me)
         def _():
@@ -331,17 +396,28 @@
         return carry
 
     lax.fori_loop(0, n_cp, src_step, 0)
+
+    forward_copy().wait_send()
 
     def done_step(src, carry):
         @pl.when(src != me)
         def _():
-            give_copy(src).wait_send()
+            @pl.when(src == relay_dst)
+            def _():
+                relay_copy().wait_send()
+
+            @pl.when(src != relay_dst)
+            def _():
+                give_copy(src).wait_send()
+
             back_copy(src).wait_send()
             back_wait(src)
 
         return carry
 
     lax.fori_loop(0, n_cp, done_step, 0)
+
+    load.wait()
 
     def col_step(col, carry):
         slot = lax.rem(col, 2)
@@ -386,6 +462,7 @@
             scratch_shapes=[
                 vmem((n_tok, d_model), BF16), vmem((n_tok, d_model), BF16), vmem((n_tok, d_model), BF16),
                 vmem((n_tok, width), BF16), vmem((2 * n_tok, width), BF16), vmem((2 * n_tok, width), BF16),
+                vmem((n_tok // 2, head_dim), BF16), vmem((n_tok // 2, head_dim), BF16),
                 vmem((2, 3, d_model, head_dim), BF16), vmem((2, 2, d_model, head_dim), BF16), vmem((2, width, N_COLS), BF16),
                 dma, dma((2, 3)), dma((2, 2)), dma((2,)), dma((2,)), dma((2,)), pltpu.SemaphoreType.REGULAR((2,)),
             ],
@@ -393,18 +470,18 @@
             cost_estimate=pl.CostEstimate(flops=5 * 7 * flops, bytes_accessed=5 * 63 * 2 ** 20, transcendentals=0),
             name="local_layers",
         )(hidden, *w_heads, w_flat)
-        order = sorted(range(1, n_cp), key=lambda off: (-min(off, n_cp - off), off)) + [0]
+        n_grp = n_tok // Q_ROWS
         return pl.pallas_call(
-            functools.partial(global_layer, n_cp, n_layers - 1, order, dims),
+            functools.partial(global_layer, n_cp, n_layers - 1, dims),
             out_shape=jax.ShapeDtypeStruct(hidden.shape, hidden.dtype),
             in_specs=[any_spec] * 5, out_specs=any_spec,
             scratch_shapes=[
-                vmem((n_tok, d_model), BF16), vmem((n_tok, d_model), BF16),
+                vmem((n_tok, d_model), BF16),
                 vmem((n_heads, 3, n_tok, head_dim), BF16), vmem((n_cp, 3, n_tok, head_dim), BF16),
-                vmem((n_cp, n_tok, head_dim), BF16), vmem((n_tok, width), BF16),
+                vmem((3, n_tok, head_dim), BF16), vmem((n_cp, n_tok, head_dim), BF16), vmem((n_tok, width), BF16),
                 vmem((2, 3, d_model, head_dim), BF16), vmem((2, width, N_COLS), BF16),
-                vmem((G_ROWS, 128), F32), vmem((G_ROWS, 128), F32), vmem((G_ROWS, head_dim), F32),
-                dma, dma((2, 3)), dma((2,)), dma((n_cp,)), dma((n_cp,)), dma((n_cp,)), dma((n_cp,)),
+                *[vmem((Q_ROWS, 128), F32)] * (2 * n_grp), *[vmem((Q_ROWS, head_dim), F32)] * n_grp,
+                dma, dma((2, 3)), dma((2,)), dma((n_cp,)), dma((n_cp,)), dma((n_cp,)), dma((n_cp,)), dma, dma,
             ],
             compiler_params=pltpu.CompilerParams(collective_id=1, has_side_effects=True, vmem_limit_bytes=big),
             cost_estimate=pl.CostEstimate(flops=8 * flops, bytes_accessed=63 * 2 ** 20, transcendentals=0),

time: 1200 us -> 934 us (0.78)
  Pallas kernels: 1050 us -> 789 us
    pallas_call x1, Pallas kernels: 662 us -> 520 us  [device_body(): pl.pallas_call(functools.partial(local_layers, n_cp, n_layers - 1, dims),...]
    pallas_call x1, Pallas kernels: 391 us -> 269 us  [device_body(): pl.pallas_call(functools.partial(global_layer, n_cp, n_layers - 1, dims),...]
where the time goes in v2:
time: 934 us; the launch traced here: 918 us
  Pallas kernels  789 us (84%)
  local copies, waits for them, and re-layouts  129 us (14%)
    pallas_call x1, Pallas kernels, device_body(): pl.pallas_call(functools.partial(local_layers, n_cp, n_layers - 1, dims),...  520 us
    pallas_call x1, Pallas kernels, device_body(): pl.pallas_call(functools.partial(global_layer, n_cp, n_layers - 1, dims),...  269 us
    transpose x1, local copies, waits for them, and re-layouts, device_body(): jnp.transpose(w, (0, 2, 1, 3))  82.1 us
    unnamed x2, local copies, waits for them, and re-layouts  46.6 us

profile of v2, /device:TPU:113, one launch (start us, length us, event | category | flops | bytes accessed | tf_op | source)
XLA Modules:
  0.0 917.9 jit_solution(8380847479321816956)
XLA Ops:
  0.0 41.5 %copy.12 = bf16[6,2560,8,256]{3,1,2,0:T(8,128)(2,1)} copy(bf16[6,2560,8,256]{3,2,1,0:T(8,128)(2,1)} %param.6) | data formatting | bytes 125829120 | tf_op args[1]
  41.5 82.1 %copy_bitcast_fusion = (bf16[6,8,2560,256]{3,2,1,0:T(8,128)(2,1)}, bf16[6,8,2560,256]{3,2,1,0:T(8,128)(2,1)}) fusion(bf16[6,2560,8,256]{3,2,1,0:T(8,128)(2,1)} %param.8, bf16[6,2560,8,256]{3,2,1,0:T(8,128)(2,1)} %param.7), kind=kLoop, calls=%fused_computation | loop fusion | bytes 251658240 | tf_op jit(solution)/shard_map/transpose | solution.py:451
  123.6 520.1 %local_layers.1.x_hbm = bf16[1024,2560]{1,0:T(8,128)(2,1)} custom-call(bf16[1024,2560]{1,0:T(8,128)(2,1)} %x_hbm.1, bf16[6,8,2560,256]{3,2,1,0:T(8,128)(2,1)} %bitcast.8, bf16[6,8,2560,256]{3,2,1,0:T(8,128)(2,1)} %get-tuple-element.6.wk_hbm, bf16[6,8,2560,256]{3,2,1,0:T(8,128)(2,1)} %get-tuple-element.5.wv_hbm, bf16[6,2048,2560]{2,1,0:T(8,128)(2,1)} %bitcast.10), custom_call_target="tpu_custom_call" | custom-call | flops 375809638400 | bytes 330301440 | tf_op jit(solution)/shard_map/local_layers/pallas_call | solution.py:458
  643.6 269.0 %global_layer.1 = bf16[1024,2560]{1,0:T(8,128)(2,1)} custom-call(bf16[1024,2560]{1,0:T(8,128)(2,1)} %local_layers.1.x_hbm, bf16[6,8,2560,256]{3,2,1,0:T(8,128)(2,1)} %bitcast.9, bf16[6,8,2560,256]{3,2,1,0:T(8,128)(2,1)} %get-tuple-element.6.wk_hbm, bf16[6,8,2560,256]{3,2,1,0:T(8,128)(2,1)} %get-tuple-element.5.wv_hbm, bf16[6,2048,2560]{2,1,0:T(8,128)(2,1)} %bitcast.11), custom_call_target="tpu_custom_call" | custom-call | flops 85899345920 | bytes 66060288 | tf_op jit(solution)/shard_map/global_layer/pallas_call | solution.py:474
  912.7 5.2 copy.14

commit v3 on v2

--- a/solution.py
+++ b/solution.py
@@ -225,23 +225,19 @@
 
 
 def global_layer(n_cp, layer, dims, x_hbm, wq_hbm, wk_hbm, wv_hbm, wo_hbm, out_hbm,
-                 x_ref, stage, held, relay, o_stage, o_all, w_own, w_out, *rest):
+                 x_ref, stage, held, o_stage, o_all, w_own, w_out, *rest):
     n_tok, d_model, n_heads, head_dim = dims
     half = n_tok // 2
     n_cols = d_model // N_COLS
     exp_scale = head_dim ** -0.5 * math.log2(math.e)
     n_grp = n_tok // Q_ROWS
     run_max, run_sum, acc = rest[:n_grp], rest[n_grp:2 * n_grp], rest[2 * n_grp:3 * n_grp]
-    io_sem, own_sem, out_sem, send_sem, recv_sem, o_send, o_recv, relay_send, relay_recv = rest[3 * n_grp:]
+    io_sem, own_sem, out_sem, send_sem, recv_sem, o_send, o_recv = rest[3 * n_grp:]
     me = lax.axis_index("cp")
     w_in = (wq_hbm, wk_hbm, wv_hbm)
     mate = me + 1 - 2 * lax.rem(me, 2)
     far, back = n_cp // 2, n_cp - 2
-    via = lax.rem(me + back, n_cp)
-    relay_dst = lax.rem(mate + far, n_cp)
-    relay_src = lax.rem(me + 2, n_cp)
-    relay_end = lax.rem(mate + back, n_cp)
-    peers = [relay_dst, lax.rem(me + far, n_cp), lax.rem(me + 2, n_cp), lax.rem(me + back, n_cp),
+    peers = [lax.rem(mate + far, n_cp), lax.rem(me + far, n_cp), lax.rem(me + 2, n_cp), lax.rem(me + back, n_cp),
              lax.rem(mate + 2, n_cp), lax.rem(mate + back, n_cp), mate, me]
 
     def peer(step):
@@ -259,16 +255,6 @@
     def give_copy(dst):
         return pltpu.make_async_remote_copy(src_ref=stage.at[dst], dst_ref=held.at[me], send_sem=send_sem.at[dst],
                                             recv_sem=recv_sem.at[me], device_id={"cp": dst},
-                                            device_id_type=pl.DeviceIdType.MESH)
-
-    def relay_copy():
-        return pltpu.make_async_remote_copy(src_ref=stage.at[relay_dst], dst_ref=relay, send_sem=send_sem.at[relay_dst],
-                                            recv_sem=relay_recv, device_id={"cp": via},
-                                            device_id_type=pl.DeviceIdType.MESH)
-
-    def forward_copy():
-        return pltpu.make_async_remote_copy(src_ref=relay, dst_ref=held.at[relay_src], send_sem=relay_send,
-                                            recv_sem=recv_sem.at[relay_src], device_id={"cp": relay_end},
                                             device_id_type=pl.DeviceIdType.MESH)
 
     def take_wait(src):
@@ -314,11 +300,7 @@
                 stage[head, which, pl.ds(part * half, half), :] = dot_nn(
                     x_ref[pl.ds(part * half, half), :], w_own[slot, which]).astype(BF16)
 
-        @pl.when(step == 0)
-        def _():
-            relay_copy().start()
-
-        @pl.when((step > 0) & (step + 1 < n_heads))
+        @pl.when(step + 1 < n_heads)
         def _():
             give_copy(head).start()
 
@@ -326,8 +308,6 @@
 
     lax.fori_loop(0, n_heads, own_step, 0)
     load.start()
-    relay_copy().wait_recv()
-    forward_copy().start()
 
     def keep_step(idx, carry):
         rows = aligned(idx * 128, 128)
@@ -397,18 +377,11 @@
 
     lax.fori_loop(0, n_cp, src_step, 0)
 
-    forward_copy().wait_send()
 
     def done_step(src, carry):
         @pl.when(src != me)
         def _():
-            @pl.when(src == relay_dst)
-            def _():
-                relay_copy().wait_send()
-
-            @pl.when(src != relay_dst)
-            def _():
-                give_copy(src).wait_send()
+            give_copy(src).wait_send()
 
             back_copy(src).wait_send()
             back_wait(src)
@@ -478,10 +451,10 @@
             scratch_shapes=[
                 vmem((n_tok, d_model), BF16),
                 vmem((n_heads, 3, n_tok, head_dim), BF16), vmem((n_cp, 3, n_tok, head_dim), BF16),
-                vmem((3, n_tok, head_dim), BF16), vmem((n_cp, n_tok, head_dim), BF16), vmem((n_tok, width), BF16),
+                vmem((n_cp, n_tok, head_dim), BF16), vmem((n_tok, width), BF16),
                 vmem((2, 3, d_model, head_dim), BF16), vmem((2, width, N_COLS), BF16),
                 *[vmem((Q_ROWS, 128), F32)] * (2 * n_grp), *[vmem((Q_ROWS, head_dim), F32)] * n_grp,
-                dma, dma((2, 3)), dma((2,)), dma((n_cp,)), dma((n_cp,)), dma((n_cp,)), dma((n_cp,)), dma, dma,
+                dma, dma((2, 3)), dma((2,)), dma((n_cp,)), dma((n_cp,)), dma((n_cp,)), dma((n_cp,)),
             ],
             compiler_params=pltpu.CompilerParams(collective_id=1, has_side_effects=True, vmem_limit_bytes=big),
             cost_estimate=pl.CostEstimate(flops=8 * flops, bytes_accessed=63 * 2 ** 20, transcendentals=0),

time: 934 us -> 909 us (0.973); the launches traced: 918 us -> 908 us
  Pallas kernels: 789 us -> 779 us
    pallas_call x1, Pallas kernels: 269 us -> 259 us  [device_body(): pl.pallas_call(functools.partial(global_layer, n_cp, n_layers - 1, dims),...]
where the time goes in v3:
time: 909 us; the launch traced here: 908 us
  Pallas kernels  779 us (86%)
  local copies, waits for them, and re-layouts  129 us (14%)
    pallas_call x1, Pallas kernels, device_body(): pl.pallas_call(functools.partial(local_layers, n_cp, n_layers - 1, dims),...  520 us
    pallas_call x1, Pallas kernels, device_body(): pl.pallas_call(functools.partial(global_layer, n_cp, n_layers - 1, dims),...  259 us
    transpose x1, local copies, waits for them, and re-layouts, device_body(): jnp.transpose(w, (0, 2, 1, 3))  82.1 us
    unnamed x2, local copies, waits for them, and re-layouts  46.6 us

profile of v3, /device:TPU:113, one launch (start us, length us, event | category | flops | bytes accessed | tf_op | source)
XLA Modules:
  0.0 907.6 jit_solution(1737063656790929552)
XLA Ops:
  0.0 41.5 %copy.12 = bf16[6,2560,8,256]{3,1,2,0:T(8,128)(2,1)} copy(bf16[6,2560,8,256]{3,2,1,0:T(8,128)(2,1)} %param.6) | data formatting | bytes 125829120 | tf_op args[1]
  41.5 82.1 %copy_bitcast_fusion = (bf16[6,8,2560,256]{3,2,1,0:T(8,128)(2,1)}, bf16[6,8,2560,256]{3,2,1,0:T(8,128)(2,1)}) fusion(bf16[6,2560,8,256]{3,2,1,0:T(8,128)(2,1)} %param.8, bf16[6,2560,8,256]{3,2,1,0:T(8,128)(2,1)} %param.7), kind=kLoop, calls=%fused_computation | loop fusion | bytes 251658240 | tf_op jit(solution)/shard_map/transpose | solution.py:424
  123.6 520.1 %local_layers.1.x_hbm = bf16[1024,2560]{1,0:T(8,128)(2,1)} custom-call(bf16[1024,2560]{1,0:T(8,128)(2,1)} %x_hbm.1, bf16[6,8,2560,256]{3,2,1,0:T(8,128)(2,1)} %bitcast.8, bf16[6,8,2560,256]{3,2,1,0:T(8,128)(2,1)} %get-tuple-element.6.wk_hbm, bf16[6,8,2560,256]{3,2,1,0:T(8,128)(2,1)} %get-tuple-element.5.wv_hbm, bf16[6,2048,2560]{2,1,0:T(8,128)(2,1)} %bitcast.10), custom_call_target="tpu_custom_call" | custom-call | flops 375809638400 | bytes 330301440 | tf_op jit(solution)/shard_map/local_layers/pallas_call | solution.py:431
  643.6 258.8 %global_layer.1 = bf16[1024,2560]{1,0:T(8,128)(2,1)} custom-call(bf16[1024,2560]{1,0:T(8,128)(2,1)} %local_layers.1.x_hbm, bf16[6,8,2560,256]{3,2,1,0:T(8,128)(2,1)} %bitcast.9, bf16[6,8,2560,256]{3,2,1,0:T(8,128)(2,1)} %get-tuple-element.6.wk_hbm, bf16[6,8,2560,256]{3,2,1,0:T(8,128)(2,1)} %get-tuple-element.5.wv_hbm, bf16[6,2048,2560]{2,1,0:T(8,128)(2,1)} %bitcast.11), custom_call_target="tpu_custom_call" | custom-call | flops 85899345920 | bytes 66060288 | tf_op jit(solution)/shard_map/global_layer/pallas_call | solution.py:447
  902.5 5.2 copy.14
